TPU v7x, 32 devices: a whole 2x2x4 slice. The times are simulated.
32 devices in a mesh: copy: 4 (over z), row: 4 (over x, core), col: 2 (over y).
Axes of the slice: x: 2, y: 2, z: 4, core: 2. Of those that a mesh axis runs over, the one named last changes fastest.
Arguments:
- trailing: float32 [32768, 16, 2, 128], P(('copy', 'row'), None, 'col'), parts along dimension 0, may hold values from -6 to 6
- lower_trail: float32 [64, 2, 128, 768], P(('copy', 'row'), None, None, 'col'), parts along dimension 0, may hold values from -0.09375 to 0.09375
- lower_cross: float32 [384, 384], replicated, may hold values from -0.3125 to 0.3125
- panel_inverse: float32 [2, 384, 384], replicated, may hold values from -1 to 1, as said below
- target: float32 [32768, 2, 384], P(('copy', 'row'), None, 'col'), parts along dimension 0, may hold values from -6 to 6
Outputs:
- inverse_panels: float32 [32768, 2, 384], P(('copy', 'row'), None, 'col'), parts along dimension 0
There are 4 independent parts, one for each index of `copy`. A program takes and returns all parts, laid end to end along the dimension named above; an argument that names none is the same for every part. Nothing has to cross between parts.
Inputs may be any that keep to these rules, and one draw needn't show every extreme that they name: `panel_inverse`: each of the two 384 x 384 matrices is unit lower triangular: ones on the diagonal, zeros above it.
All inputs are finite; a program needn't handle non-finite values.
Results may differ from a plain program's by a relative error of at most 0.000071.
Values sent between devices are 32-bit elements; how exact they have to be, the bound alone decides.
A program may use at most 192 MiB of HBM per device.

v0:
```python
import jax
import jax.numpy as jnp
from jax import lax
from jax.sharding import PartitionSpec as P

precise = lax.Precision.HIGHEST


def matmul(first, second):
    return jnp.dot(first, second, preferred_element_type=jnp.float32, precision=precise)


def own_columns(matrix, dim):
    share_cols = matrix.shape[dim] // lax.axis_size("col")
    return lax.dynamic_slice_in_dim(matrix, lax.axis_index("col") * share_cols, share_cols, dim)


def per_device(trailing, lower_trail, lower_cross, panel_inverse, target):
    row_count = trailing.shape[0]
    block_cols = trailing.shape[3]
    trail_flat = trailing.reshape(row_count, trailing.shape[1] * block_cols)
    span_cols = lower_trail.shape[3] * lax.axis_size("col")
    panel_cols = span_cols // 2
    relaid = lax.all_to_all(lower_trail, "col", split_axis=1, concat_axis=3, tiled=True)
    segment = lax.all_gather(relaid, "row", axis=0, tiled=True)
    block_count = segment.shape[0]
    update = matmul(trail_flat, segment.reshape(block_count * block_cols, span_cols))
    update = update.reshape(row_count, 2, panel_cols)
    right_sum = lax.psum_scatter(update[:, 1], "col", scatter_dimension=1, tiled=True)
    right_rest = lax.all_gather(target[:, 1] - right_sum, "col", axis=1, tiled=True)
    right_panel = matmul(right_rest, panel_inverse[1])
    left_sum = lax.psum_scatter(update[:, 0], "col", scatter_dimension=1, tiled=True)
    left_rest = lax.all_gather(target[:, 0] - left_sum, "col", axis=1, tiled=True)
    left_panel = matmul(left_rest - matmul(right_panel, lower_cross), panel_inverse[0])
    return own_columns(jnp.stack([left_panel, right_panel], axis=1), 2)


def solution(mesh):
    placed = (
        P(("copy", "row"), None, "col", None),
        P(("copy", "row"), None, None, "col"),
        P(),
        P(),
        P(("copy", "row"), None, "col"),
    )
    return jax.shard_map(
        per_device,
        mesh=mesh,
        in_specs=placed,
        out_specs=P(("copy", "row"), None, "col"),
        check_vma=False,
    )
```

profile of v0, /device:TPU:0, one launch (start us, length us, event | category | flops | bytes accessed | tf_op | source)
XLA Modules:
  0.0 366.6 jit_solution(11289346331029031825)
XLA Ops:
  6.5 0.0 copy-start
  6.5 0.0 all-gather.4.cloned.1.call-start
  6.5 1.9 copy.17
  8.5 23.3 %all_to_all.18 = f32[4,2,128,384]{2,3,0,1:T(8,128)S(1)} all-to-all(f32[4,2,128,384]{2,3,0,1:T(8,128)S(1)} %copy.17), channel_id=1, replica_groups=mesh['copy'=4,'row'=4,'col'=2] {'col'}, dimensions={1} | all-to-all | bytes 3145728 | tf_op jit(solution)/shard_map/all_to_all | solution.py:24
  31.7 0.1 copy.18
  31.9 1.6 copy.19
  33.5 0.0 all-gather.4.cloned.1.call-update
  33.5 0.0 reduce-scatter.9.cloned.1.call-start
  33.5 0.5 broadcast.3
  34.1 50.0 %reduce.3 = f32[2048,16,128]{2,1,0:T(8,128)} reduce(f32[2048,16,1,128]{3,2,1,0:T(1,128)} %param.5, f32[]{:T(128)} %broadcast.3), dimensions={2}, to_apply=%param.5.reduce_sub_computation.3 | reduce | bytes 33554436 | tf_op args[0]
  84.1 18.0 %reshape.10 = f32[2048,2048,1]{1,0,2:T(8,128)} reshape(f32[2048,16,128]{2,1,0:T(8,128)} %reduce.3) | data formatting | bytes 33554432 | tf_op jit(solution)/shard_map/reshape | solution.py:21
  102.1 0.0 all-gather.4.cloned.1.call-done
  102.1 6.6 %copy.20 = f32[768,2048]{1,0:T(8,128)} copy(f32[768,2048]{0,1:T(8,128)} %bitcast.38) | data formatting | bytes 12582912 | tf_op jit(solution)/shard_map/dot_general | solution.py:10
  108.7 49.2 %fusion.12 = f32[2048,2,384]{2,0,1:T(8,128)S(1)} fusion(f32[2048,2048,1]{1,0,2:T(8,128)} %reshape.10, f32[2,384,2048]{2,1,0:T(8,128)} %bitcast.39), kind=kOutput, calls=%fused_computation.16 | convolution fusion | flops 38654705664 | bytes 29360128 | tf_op jit(solution)/shard_map/dot_general | solution.py:10
  157.9 3.1 slice_bitcast_fusion
  161.1 3.6 copy.27
  164.6 0.0 reduce-scatter.9.cloned.1.call-update
  164.7 0.0 reduce-scatter.7.cloned.1.call-start
  164.7 3.5 copy.25
  168.3 0.0 reduce-scatter.7.cloned.1.call-update
  168.3 0.0 all-gather.8.cloned.1.call-start
  168.3 4.1 %fusion.11 = (f32[2048,1,192]{0,2,1:T(8,128)}, f32[2048,1,192]{0,2,1:T(8,128)}) fusion(f32[2048,2,192]{0,2,1:T(8,128)} %param.9), kind=kLoop, calls=%fused_computation.15 | loop fusion | bytes 6291456 | tf_op jit(solution)/shard_map/slice | solution.py:30
  172.5 1.9 copy.30
  174.3 34.4 %reduce-scatter.9.cloned.1.call-done = f32[192,2048]{1,0:T(8,128)} async-done(((f32[384,2048]{1,0:T(8,128)}), f32[192,2048]{1,0:T(8,128)}) %reduce-scatter.9.cloned.1.call-update) | async-done | bytes 1572880
  208.7 2.8 copy.28
  211.6 3.2 bitcast_subtract_fusion
  214.7 2.8 copy.23
  217.6 0.0 all-gather.8.cloned.1.call-update
  217.6 0.0 all-gather.6.cloned.1.call-start
  217.6 2.0 copy.29
  219.6 34.8 %reduce-scatter.7.cloned.1.call-done = f32[192,2048]{1,0:T(8,128)} async-done(((f32[384,2048]{1,0:T(8,128)}), f32[192,2048]{1,0:T(8,128)}) %reduce-scatter.7.cloned.1.call-update) | async-done | bytes 1572880
  254.5 2.8 copy.26
  257.2 3.2 bitcast_subtract_fusion.1
  260.4 0.0 copy-start.3
  260.4 3.0 copy.21
  263.4 0.0 all-gather.6.cloned.1.call-update
  263.5 37.3 %all-gather.8.cloned.1.call-done = f32[2048,384]{0,1:T(8,128)} async-done(((f32[2048,192]{0,1:T(8,128)}), f32[2048,384]{0,1:T(8,128)}) %all-gather.8.cloned.1.call-update) | async-done | bytes 3145744 | tf_op jit(solution)/shard_map/all_gather | solution.py:30
  300.8 0.0 copy-done.3
  300.8 7.3 %fusion.7 = f32[2048,384]{0,1:T(8,128)S(1)} fusion(f32[2048,384]{0,1:T(8,128)} %all-gather.8.cloned.1.call-done, f32[2,384,384]{2,1,0:T(8,128)S(1)} %copy-done.3), kind=kOutput, calls=%fused_computation.11 | convolution fusion | flops 3623878656 | bytes 6881280 | tf_op jit(solution)/shard_map/dot_general | solution.py:10
  308.1 0.0 copy-start.1
  308.1 1.7 copy-done.1
  309.8 0.0 copy-done
  309.8 8.2 %fusion.13 = f32[2048,384]{1,0:T(8,128)} fusion(f32[2048,384]{0,1:T(8,128)S(1)} %fusion.7, f32[384,384]{1,0:T(8,128)S(1)} %copy-done), kind=kOutput, calls=%fused_computation.17 | convolution fusion | flops 3623878656 | bytes 6881280 | tf_op jit(solution)/shard_map/dot_general | solution.py:10
  318.0 29.2 %all-gather.6.cloned.1.call-done = f32[2048,384]{0,1:T(8,128)} async-done(((f32[2048,192]{0,1:T(8,128)}), f32[2048,384]{0,1:T(8,128)}) %all-gather.6.cloned.1.call-update) | async-done | bytes 3145744 | tf_op jit(solution)/shard_map/all_gather | solution.py:33
  347.1 3.5 copy.24
  350.7 7.5 %fusion.3 = f32[2048,1,384]{0,2,1:T(8,128)S(1)} fusion(f32[2048,384]{1,0:T(8,128)} %copy.24, f32[2048,384]{1,0:T(8,128)} %fusion.13, f32[2,384,384]{2,1,0:T(8,128)S(1)} %copy-done.3), kind=kOutput, calls=%fused_computation.7 | convolution fusion | flops 3624665088 | bytes 10027008 | tf_op jit(solution)/shard_map/dot_general | solution.py:10
  358.2 0.0 copy-done.2
  358.2 1.9 fusion
  (1 shorter events, 0.0 us)
Async XLA Ops:
  6.5 303.3 %copy-start = (f32[384,384]{1,0:T(8,128)S(1)}, f32[384,384]{1,0:T(8,128)}, u32[]{:S(2)}) copy-start(f32[384,384]{1,0:T(8,128)} %param.7) | copy-start | bytes 1769476
  6.5 95.6 %all-gather.4.cloned.1.call-start = ((), (), s32[]{:S(2)}) async-start(), calls=%async_computation.3 | async-start | bytes 7864320 | tf_op jit(solution)/shard_map/all_gather | solution.py:25
  33.5 175.2 %reduce-scatter.9.cloned.1.call-start = ((), (), s32[]{:S(2)}) async-start(), calls=%async_computation.7 | async-start | bytes 4718592
  164.7 89.8 %reduce-scatter.7.cloned.1.call-start = ((), (), s32[]{:S(2)}) async-start(), calls=%async_computation.6 | async-start | bytes 4718592
  168.3 132.5 %all-gather.8.cloned.1.call-start = ((), (), s32[]{:S(2)}) async-start(), calls=%async_computation.5 | async-start | bytes 4718592 | tf_op jit(solution)/shard_map/all_gather | solution.py:30
  217.6 129.5 %all-gather.6.cloned.1.call-start = ((), (), s32[]{:S(2)}) async-start(), calls=%async_computation.4 | async-start | bytes 4718592 | tf_op jit(solution)/shard_map/all_gather | solution.py:33
  260.4 40.4 %copy-start.3 = (f32[2,384,384]{2,1,0:T(8,128)S(1)}, f32[2,384,384]{2,1,0:T(8,128)}, u32[]{:S(2)}) copy-start(f32[2,384,384]{2,1,0:T(8,128)} %param.8) | copy-start | bytes 3538948
  308.1 1.7 copy-start.1
  350.7 7.5 %copy-start.2 = (f32[2048,384]{0,1:T(8,128)S(1)}, f32[2048,384]{0,1:T(8,128)}, u32[]{:S(2)}) copy-start(f32[2048,384]{0,1:T(8,128)} %copy-done.1) | copy-start | bytes 9437188
Sparse Core Ops, SparseCore 0:
  33.6 46.8 all-gather.3
  164.8 43.8 reduce-scatter.8
  211.0 43.4 reduce-scatter.6
  255.9 44.9 all-gather.7
  302.2 44.8 all-gather.5
where the time goes:
time: 368 us; the launch traced here: 367 us
  waiting for transfers between devices  136 us (37%)
  matrix products  72.2 us (20%)
  local copies, waits for them, and re-layouts  63.7 us (17%)
  other arithmetic  58.3 us (16%)
  blocking collectives  23.3 us (6%)
  between operations  13.2 us (4%)
    dot_general x4, matrix products, matmul(): jnp.dot(first, second, preferred_element_type=jnp.float32, precision=prec...  72.2 us
    unnamed x7, waiting for transfers between devices  69.3 us
    unnamed x1, other arithmetic  50 us
    all_gather x1, waiting for transfers between devices, per_device(): lax.all_gather(target[:, 1] - right_sum, 'col', axis=1, tiled=True)  37.3 us
    all_gather x1, waiting for transfers between devices, per_device(): lax.all_gather(target[:, 0] - left_sum, 'col', axis=1, tiled=True)  29.2 us
    all_to_all x1, blocking collectives, per_device(): lax.all_to_all(lower_trail, 'col', split_axis=1, concat_axis=3, tiled=True)  23.3 us
    unnamed x16, local copies, waits for them, and re-layouts  20.7 us
    reshape x1, local copies, waits for them, and re-layouts, per_device(): trail_flat = trailing.reshape(row_count, trailing.shape[1] * block_cols)  18 us
  transfers between devices with their start and end apart: 5, of which 4 were waited for; matrix products, arithmetic and copies ran while one was open for 31% of the time, Pallas kernels for 0%

commit v1 on v0

--- a/solution.py
+++ b/solution.py
@@ -21,7 +21,9 @@
     trail_flat = trailing.reshape(row_count, trailing.shape[1] * block_cols)
     span_cols = lower_trail.shape[3] * lax.axis_size("col")
     panel_cols = span_cols // 2
-    relaid = lax.all_to_all(lower_trail, "col", split_axis=1, concat_axis=3, tiled=True)
+    parts = jnp.split(lower_trail, lax.axis_size("col"), axis=1)
+    received = lax.all_to_all(jnp.stack(parts), "col", 0, 0)
+    relaid = jnp.concatenate(received, axis=3)
     segment = lax.all_gather(relaid, "row", axis=0, tiled=True)
     block_count = segment.shape[0]
     update = matmul(trail_flat, segment.reshape(block_count * block_cols, span_cols))

time: 368 us -> 384 us (1.043)
  waiting for transfers between devices: 136 us -> 212 us
  local copies, waits for them, and re-layouts: 63.7 us -> 9.96 us
  other arithmetic: 58.3 us -> 7.16 us
  matrix products: 72.2 us -> 115 us
    reduce_scatter x0 -> x2, waiting for transfers between devices: none -> 88.5 us  [the longest x1 45.7 us: per_device(): lax.psum_scatter(update[:, 1], 'col', scatter_dimension=1, tiled=True)]
    unnamed x7 -> x5, waiting for transfers between devices: 69.3 us -> 1.26 us
    unnamed x1 -> x0, other arithmetic: 50 us -> none
    all_gather x1, waiting for transfers between devices: 0.01 us -> 46.9 us  [per_device(): segment = lax.all_gather(relaid, 'row', axis=0, tiled=True)]
    dot_general x4, matrix products: 72.2 us -> 115 us  [matmul(): jnp.dot(first, second, preferred_element_type=jnp.float32, precision=prec...]
    unnamed x16 -> x8, local copies, waits for them, and re-layouts: 20.7 us -> 1.69 us
    reshape x1 -> x2, local copies, waits for them, and re-layouts: 18 us -> 3.61 us  [per_device(): relaid = jnp.concatenate(received, axis=3)]
    all_gather x1, waiting for transfers between devices: 37.3 us -> 44.5 us  [per_device(): lax.all_gather(target[:, 1] - right_sum, 'col', axis=1, tiled=True)]
  transfers between devices with their start and end apart: 5 -> 5, of which waited for: 4 -> 5; matrix products, arithmetic and copies ran while one was open for 31% -> 4% of each run, Pallas kernels for 0% -> 0%
where the time goes in v1:
time: 384 us; the launch traced here: 381 us
  waiting for transfers between devices  212 us (55%)
  matrix products  115 us (30%)
  blocking collectives  23.3 us (6%)
  between operations  13.4 us (3%)
  local copies, waits for them, and re-layouts  9.96 us (3%)
  other arithmetic  7.16 us (2%)
    dot_general x4, matrix products, matmul(): jnp.dot(first, second, preferred_element_type=jnp.float32, precision=prec...  115 us
    all_gather x1, waiting for transfers between devices, per_device(): segment = lax.all_gather(relaid, 'row', axis=0, tiled=True)  46.9 us
    reduce_scatter x1, waiting for transfers between devices, per_device(): lax.psum_scatter(update[:, 1], 'col', scatter_dimension=1, tiled=True)  45.7 us
    all_gather x1, waiting for transfers between devices, per_device(): lax.all_gather(target[:, 1] - right_sum, 'col', axis=1, tiled=True)  44.5 us
    reduce_scatter x1, waiting for transfers between devices, per_device(): lax.psum_scatter(update[:, 0], 'col', scatter_dimension=1, tiled=True)  42.8 us
    all_gather x1, waiting for transfers between devices, per_device(): lax.all_gather(target[:, 0] - left_sum, 'col', axis=1, tiled=True)  30.4 us
    all_to_all x1, blocking collectives, per_device(): received = lax.all_to_all(jnp.stack(parts), 'col', 0, 0)  23.3 us
  transfers between devices with their start and end apart: 5, of which 5 were waited for; matrix products, arithmetic and copies ran while one was open for 4% of the time, Pallas kernels for 0%

profile of v1, /device:TPU:0, one launch (start us, length us, event | category | flops | bytes accessed | tf_op | source)
XLA Modules:
  0.0 380.9 jit_solution(13763871465259631258)
XLA Ops:
  6.5 0.0 copy-start
  6.5 0.0 all-gather.4.cloned.1.call-start
  6.5 1.5 slice_bitcast_fusion.3
  8.1 0.1 pad_maximum_fusion
  8.2 23.3 %all_to_all.5 = f32[2,4,1,128,384]{4,3,1,2,0:T(8,128)S(1)} all-to-all(f32[2,4,1,128,384]{4,3,1,2,0:T(8,128)S(1)} %pad_maximum_fusion), channel_id=1, replica_groups=mesh['copy'=4,'row'=4,'col'=2] {'col'}, dimensions={0} | all-to-all | bytes 3145728 | tf_op jit(solution)/shard_map/all_to_all | solution.py:25
  31.5 1.2 copy.10
  32.7 2.4 reshape.18
  35.1 0.0 all-gather.4.cloned.1.call-update
  35.1 0.0 reduce-scatter.3.cloned.1.call-start
  35.2 46.9 %all-gather.4.cloned.1.call-done = f32[16,1,128,768]{3,2,1,0:T(8,128)} async-done(((f32[4,1,128,768]{3,2,1,0:T(8,128)}), f32[16,1,128,768]{3,2,1,0:T(8,128)}) %all-gather.4.cloned.1.call-update) | async-done | bytes 6291472 | tf_op jit(solution)/shard_map/all_gather | solution.py:27
  82.1 93.6 %fusion = f32[768,2048,1]{1,0,2:T(8,128)S(1)} fusion(f32[2048,16,128]{2,1,0:T(8,128)} %bitcast.42, f32[16,1,128,768]{3,2,1,0:T(8,128)} %all-gather.4.cloned.1.call-done), kind=kOutput, calls=%fused_computation | convolution fusion | flops 38654705664 | bytes 29360128 | tf_op jit(solution)/shard_map/dot_general | solution.py:10
  175.7 3.1 slice_bitcast_fusion
  178.8 0.0 reduce-scatter.3.cloned.1.call-update
  178.9 0.0 reduce-scatter.5.cloned.1.call-start
  178.9 0.7 reduce-scatter.5.cloned.1.call-update
  179.6 0.0 all-gather.8.cloned.1.call-start
  179.6 42.8 %reduce-scatter.3.cloned.1.call-done = f32[2048,192]{0,1:T(8,128)} async-done(((f32[2048,384]{0,1:T(8,128)}), f32[2048,192]{0,1:T(8,128)}) %reduce-scatter.3.cloned.1.call-update) | async-done | bytes 1572880 | tf_op jit(solution)/shard_map/reduce_scatter | solution.py:34
  222.5 45.7 %reduce-scatter.5.cloned.1.call-done = f32[2048,192]{0,1:T(8,128)} async-done(((f32[2048,384]{0,1:T(8,128)}), f32[2048,192]{0,1:T(8,128)}) %reduce-scatter.5.cloned.1.call-update) | async-done | bytes 1572880 | tf_op jit(solution)/shard_map/reduce_scatter | solution.py:31
  268.1 5.2 %bitcast_subtract_fusion = (f32[2048,192]{0,1:T(8,128)}, f32[2048,192]{0,1:T(8,128)}) fusion(f32[2048,192]{0,1:T(8,128)} %reduce-scatter.5.cloned.1.call-done, f32[2048,2,192]{0,2,1:T(8,128)} %param.9, f32[2048,192]{0,1:T(8,128)} %reduce-scatter.3.cloned.1.call-done), kind=kLoop, calls=%fused_computation.12 | loop fusion | flops 786432 | bytes 9437184 | tf_op jit(solution)/shard_map/sub | solution.py:32
  273.3 0.0 copy-start.3
  273.3 0.0 all-gather.8.cloned.1.call-update
  273.4 0.0 all-gather.6.cloned.1.call-start
  273.4 0.5 all-gather.6.cloned.1.call-update
  273.9 44.5 %all-gather.8.cloned.1.call-done = f32[2048,384]{0,1:T(8,128)} async-done(((f32[2048,192]{0,1:T(8,128)}), f32[2048,384]{0,1:T(8,128)}) %all-gather.8.cloned.1.call-update) | async-done | bytes 3145744 | tf_op jit(solution)/shard_map/all_gather | solution.py:32
  318.4 0.0 copy-done.3
  318.4 7.3 %fusion.10 = f32[2048,384]{0,1:T(8,128)S(1)} fusion(f32[2048,384]{0,1:T(8,128)} %all-gather.8.cloned.1.call-done, f32[2,384,384]{2,1,0:T(8,128)S(1)} %copy-done.3), kind=kOutput, calls=%fused_computation.17 | convolution fusion | flops 3623878656 | bytes 6881280 | tf_op jit(solution)/shard_map/dot_general | solution.py:10
  325.8 0.0 copy-start.1
  325.8 1.7 copy-done.1
  327.4 0.0 copy-done
  327.4 6.9 %fusion.14 = f32[2048,384]{0,1:T(8,128)} fusion(f32[2048,384]{0,1:T(8,128)S(1)} %fusion.10, f32[384,384]{1,0:T(8,128)S(1)} %copy-done), kind=kOutput, calls=%fused_computation.21 | convolution fusion | flops 3623878656 | bytes 6881280 | tf_op jit(solution)/shard_map/dot_general | solution.py:10
  334.4 30.4 %all-gather.6.cloned.1.call-done = f32[2048,384]{0,1:T(8,128)} async-done(((f32[2048,192]{0,1:T(8,128)}), f32[2048,384]{0,1:T(8,128)}) %all-gather.6.cloned.1.call-update) | async-done | bytes 3145744 | tf_op jit(solution)/shard_map/all_gather | solution.py:35
  364.8 0.0 copy-start.2
  364.8 7.5 %fusion.6 = f32[2048,1,384]{0,2,1:T(8,128)S(1)} fusion(f32[2048,384]{0,1:T(8,128)} %all-gather.6.cloned.1.call-done, f32[2048,384]{0,1:T(8,128)} %fusion.14, f32[2,384,384]{2,1,0:T(8,128)S(1)} %copy-done.3), kind=kOutput, calls=%fused_computation.10 | convolution fusion | flops 3624665088 | bytes 10027008 | tf_op jit(solution)/shard_map/dot_general | solution.py:10
  372.3 0.0 copy-done.2
  372.3 1.9 fusion.3
Async XLA Ops:
  6.5 320.9 %copy-start = (f32[384,384]{1,0:T(8,128)S(1)}, f32[384,384]{1,0:T(8,128)}, u32[]{:S(2)}) copy-start(f32[384,384]{1,0:T(8,128)} %param.7) | copy-start | bytes 1769476
  6.5 75.6 %all-gather.4.cloned.1.call-start = ((), (), s32[]{:S(2)}) async-start(), calls=%async_computation.3 | async-start | bytes 7864320 | tf_op jit(solution)/shard_map/all_gather | solution.py:27
  35.1 187.3 %reduce-scatter.3.cloned.1.call-start = ((), (), s32[]{:S(2)}) async-start(), calls=%async_computation.4 | async-start | bytes 4718592 | tf_op jit(solution)/shard_map/reduce_scatter | solution.py:34
  178.9 89.3 %reduce-scatter.5.cloned.1.call-start = ((), (), s32[]{:S(2)}) async-start(), calls=%async_computation.6 | async-start | bytes 4718592 | tf_op jit(solution)/shard_map/reduce_scatter | solution.py:31
  179.6 138.8 %all-gather.8.cloned.1.call-start = ((), (), s32[]{:S(2)}) async-start(), calls=%async_computation.7 | async-start | bytes 4718592 | tf_op jit(solution)/shard_map/all_gather | solution.py:32
  273.3 45.1 %copy-start.3 = (f32[2,384,384]{2,1,0:T(8,128)S(1)}, f32[2,384,384]{2,1,0:T(8,128)}, u32[]{:S(2)}) copy-start(f32[2,384,384]{2,1,0:T(8,128)} %param.8) | copy-start | bytes 3538948
  273.4 91.4 %all-gather.6.cloned.1.call-start = ((), (), s32[]{:S(2)}) async-start(), calls=%async_computation.5 | async-start | bytes 4718592 | tf_op jit(solution)/shard_map/all_gather | solution.py:35
  325.8 1.7 copy-start.1
  364.8 7.5 %copy-start.2 = (f32[2048,384]{0,1:T(8,128)S(1)}, f32[2048,384]{0,1:T(8,128)}, u32[]{:S(2)}) copy-start(f32[2048,384]{0,1:T(8,128)} %copy-done.1) | copy-start | bytes 9437188
Sparse Core Ops, SparseCore 0:
  35.2 46.8 all-gather.3
  179.0 43.4 reduce-scatter.2
  224.7 43.3 reduce-scatter.4
  273.5 44.9 all-gather.7
  319.8 44.8 all-gather.5
